TPU v7x, 32 devices: a whole 2x2x4 slice. The times are simulated.
32 devices in a mesh: ep: 4 (over z), tp: 8 (over y, x, core).
Axes of the slice: x: 2, y: 2, z: 4, core: 2. Of those that a mesh axis runs over, the one named last changes fastest.
Arguments:
- tokens: bfloat16 [384, 3072], P('ep', 'tp'), may hold values from -6 to 6
- cotangent: bfloat16 [384, 3072], P('ep', 'tp'), may hold values from -6 to 6
- expert_ids: int32 [384, 2], P('ep'), may hold values from 0 to 3, all different within a row; in each aligned block of 96 rows (0 to 95, 96 to 191, ...) at most 80 rows name the same one
- combine_weights: float32 [384, 2], P('ep'), may hold values from 0.1 to 1
- w_gate: bfloat16 [4, 3072, 8192], P('ep', None, 'tp'), may hold values from -0.15625 to 0.15625
- w_up: bfloat16 [4, 3072, 8192], P('ep', None, 'tp'), may hold values from -0.109375 to 0.109375
- w_down: bfloat16 [4, 8192, 3072], P('ep', 'tp'), may hold values from -0.09375 to 0.09375
Outputs:
- mixed: bfloat16 [384, 3072], P('ep', 'tp')
- grad_tokens: bfloat16 [384, 3072], P('ep', 'tp')
- grad_combine: float32 [384, 2], P('ep')
- grad_gate: bfloat16 [4, 3072, 8192], P('ep', 'tp')
- grad_up: bfloat16 [4, 3072, 8192], P('ep', 'tp')
- grad_down: bfloat16 [4, 8192, 3072], P('ep', None, 'tp')
Inputs may be any that keep to these rules, and one draw needn't show every extreme that they name: `expert_ids`: each row names 2 different experts. Among the 96 rows of one index of ep, no expert is named more than 80 times, and in some such blocks one expert is named exactly 80 times.
All inputs are finite; a program needn't handle non-finite values.
Results may differ from a plain program's by a relative error of at most 0.019.
Values may be sent and summed in bfloat16 or wider, within the bound.
A program may use at most 128 MiB of HBM per device.

v0:
```python
import jax
import jax.numpy as jnp
from jax import lax
from jax.sharding import PartitionSpec as P


def silu_parts(gate_pre):
    sigma = jax.nn.sigmoid(gate_pre)
    return (gate_pre * sigma, sigma * (1.0 + gate_pre * (1.0 - sigma)))


def contract_rows(left, right):
    return lax.dot_general(
        left, right, (((0,), (0,)), ((), ())), preferred_element_type=jnp.float32
    )


def contract_cols(left, right):
    return lax.dot_general(
        left, right, (((1,), (1,)), ((), ())), preferred_element_type=jnp.float32
    )


def body(tokens, cotangent, expert_ids, combine_weights, w_gate, w_up, w_down):
    groups = lax.axis_size("ep")
    tok_rows, piece_width = tokens.shape
    chosen = expert_ids.shape[1]
    capacity = tok_rows * chosen * 5 // (3 * groups)
    buffer_rows = groups * capacity
    gate_weight = w_gate[0]
    up_weight = w_up[0]
    down_weight = w_down[0]
    hidden_width = gate_weight.shape[1]
    flat_ids = expert_ids.reshape(-1)
    onehot = (flat_ids[:, None] == jnp.arange(groups, dtype=jnp.int32)[None, :]).astype(jnp.int32)
    rank = jnp.sum((jnp.cumsum(onehot, axis=0) - onehot) * onehot, axis=1)
    slot_index = flat_ids * capacity + rank
    places = (jnp.arange(buffer_rows, dtype=jnp.int32)[:, None] == slot_index[None, :]).astype(
        jnp.bfloat16
    )
    placer = jnp.sum(
        places.reshape(buffer_rows, tok_rows, chosen).astype(jnp.float32), axis=2
    ).astype(jnp.bfloat16)
    scaled = (combine_weights[:, :, None] * cotangent[:, None, :].astype(jnp.float32)).astype(
        jnp.bfloat16
    )
    send_grad = jnp.dot(
        places, scaled.reshape(tok_rows * chosen, piece_width), preferred_element_type=jnp.float32
    ).astype(jnp.bfloat16)
    send_rows = jnp.dot(placer, tokens, preferred_element_type=jnp.float32).astype(jnp.bfloat16)
    recv_rows, recv_grad = (
        lax.all_to_all(
            send_rows.reshape(groups, capacity, piece_width),
            "ep",
            split_axis=0,
            concat_axis=0,
            tiled=True,
        ),
        lax.all_to_all(
            send_grad.reshape(groups, capacity, piece_width),
            "ep",
            split_axis=0,
            concat_axis=0,
            tiled=True,
        ),
    )
    recv_rows = recv_rows.reshape(buffer_rows, piece_width)
    piece = lax.all_gather(recv_rows, "tp", axis=1, tiled=True)
    gate_pre = jnp.dot(piece, gate_weight, preferred_element_type=jnp.float32)
    up_pre = jnp.dot(piece, up_weight, preferred_element_type=jnp.float32)
    recv_grad = recv_grad.reshape(buffer_rows, piece_width)
    active, slope = silu_parts(gate_pre)
    hidden = (active * up_pre).astype(jnp.bfloat16)
    partial_value = jnp.dot(hidden, down_weight, preferred_element_type=jnp.float32)
    out_piece = lax.psum_scatter(
        partial_value.astype(jnp.bfloat16), "tp", scatter_dimension=1, tiled=True
    )
    out_back = lax.all_to_all(
        out_piece.reshape(groups, capacity, piece_width),
        "ep",
        split_axis=0,
        concat_axis=0,
        tiled=True,
    ).reshape(buffer_rows, piece_width)
    out_tokens = (
        jnp.take(out_back, slot_index, axis=0)
        .reshape(tok_rows, chosen, piece_width)
        .astype(jnp.float32)
    )
    mixed = jnp.sum(combine_weights[:, :, None] * out_tokens, axis=1).astype(jnp.bfloat16)
    local_products = jnp.sum(cotangent.astype(jnp.float32)[:, None, :] * out_tokens, axis=2)
    grad_combine = lax.psum(local_products, "tp")
    grad_hidden = contract_cols(lax.all_gather(recv_grad, "tp", axis=1, tiled=True), down_weight)
    down_grad = contract_rows(hidden, lax.all_gather(recv_grad, "tp", axis=1, tiled=True))
    grad_gate_pre = (grad_hidden * up_pre * slope).astype(jnp.bfloat16)
    grad_up_pre = (grad_hidden * active).astype(jnp.bfloat16)
    input_partial = contract_cols(grad_gate_pre, gate_weight) + contract_cols(
        grad_up_pre, up_weight
    )
    input_piece = lax.psum_scatter(
        input_partial.astype(jnp.bfloat16), "tp", scatter_dimension=1, tiled=True
    )
    input_back = lax.all_to_all(
        input_piece.reshape(groups, capacity, piece_width),
        "ep",
        split_axis=0,
        concat_axis=0,
        tiled=True,
    ).reshape(buffer_rows, piece_width)
    grad_tokens = jnp.sum(
        jnp.take(input_back, slot_index, axis=0)
        .reshape(tok_rows, chosen, piece_width)
        .astype(jnp.float32),
        axis=1,
    ).astype(jnp.bfloat16)
    stacked = jnp.concatenate([grad_gate_pre, grad_up_pre], axis=1)
    both_grads = contract_rows(lax.all_gather(recv_rows, "tp", axis=1, tiled=True), stacked)
    gate_grad = both_grads[:, :hidden_width].astype(jnp.bfloat16)
    up_grad = both_grads[:, hidden_width:].astype(jnp.bfloat16)
    gate_rows_out, up_rows_out = (
        lax.all_to_all(gate_grad, "tp", split_axis=0, concat_axis=1, tiled=True),
        lax.all_to_all(up_grad, "tp", split_axis=0, concat_axis=1, tiled=True),
    )
    down_cols_out = lax.all_to_all(
        down_grad.astype(jnp.bfloat16), "tp", split_axis=1, concat_axis=0, tiled=True
    )
    return (
        mixed,
        grad_tokens,
        grad_combine,
        gate_rows_out[None],
        up_rows_out[None],
        down_cols_out[None],
    )


def solution(mesh):
    placed = (
        P("ep", "tp"),
        P("ep", "tp"),
        P("ep", None),
        P("ep", None),
        P("ep", None, "tp"),
        P("ep", None, "tp"),
        P("ep", "tp", None),
    )
    return jax.shard_map(
        body,
        mesh=mesh,
        in_specs=placed,
        out_specs=(
            P("ep", "tp"),
            P("ep", "tp"),
            P("ep", None),
            P("ep", "tp", None),
            P("ep", "tp", None),
            P("ep", None, "tp"),
        ),
        check_vma=False,
    )
```

profile of v0, /device:TPU:0, one launch (start us, length us, event | category | flops | bytes accessed | tf_op | source)
XLA Modules:
  0.0 508.4 jit_solution(12819426446226769640)
XLA Ops:
  7.2 0.8 copy.55
  8.2 1.2 reduce-window.6
  9.9 1.0 mul.83
  10.8 0.2 mul.84
  11.1 0.8 copy.54
  12.0 0.3 convolution_convert_fusion.2
  12.3 14.8 %all_to_all.68 = bf16[4,80,384]{2,1,0:T(8,128)(2,1)} all-to-all(bf16[4,80,384]{2,1,0:T(8,128)(2,1)S(1)} %bitcast.77), channel_id=1, replica_groups=mesh['ep'=4,'tp'=8] {'ep'}, dimensions={0} | all-to-all | bytes 491520 | tf_op jit(solution)/shard_map/all_to_all | solution.py:59
  27.5 0.3 convolution_convert_fusion.3
  27.8 10.8 %all_to_all.69 = bf16[4,80,384]{2,1,0:T(8,128)(2,1)} all-to-all(bf16[4,80,384]{2,1,0:T(8,128)(2,1)S(1)} %bitcast.78), channel_id=1, replica_groups=mesh['ep'=4,'tp'=8] {'ep'}, dimensions={0} | all-to-all | bytes 491520 | tf_op jit(solution)/shard_map/all_to_all | solution.py:52
  38.6 15.3 %all-gather.5.cloned.1.call-done = bf16[320,3072]{1,0:T(8,128)(2,1)} async-done(((bf16[320,384]{1,0:T(8,128)(2,1)}), bf16[320,3072]{1,0:T(8,128)(2,1)}) %all-gather.5.cloned.1.call-update) | async-done | bytes 1966096 | tf_op jit(solution)/shard_map/all_gather | solution.py:93
  53.9 6.7 %fusion = f32[320,1024]{1,0:T(8,128)} fusion(bf16[320,3072]{1,0:T(8,128)(2,1)} %all-gather.5.cloned.1.call-done, bf16[1,1024,3072]{2,1,0:T(8,128)(2,1)} %param.15), kind=kOutput, calls=%fused_computation.4 | convolution fusion | flops 2013265920 | bytes 9568256 | tf_op jit(solution)/shard_map/dot_general | solution.py:19
  60.6 22.8 %all-gather.3.cloned.1.call-done = bf16[320,3072]{1,0:T(8,128)(2,1)} async-done(((bf16[320,384]{1,0:T(8,128)(2,1)}), bf16[320,3072]{1,0:T(8,128)(2,1)}) %all-gather.3.cloned.1.call-update) | async-done | bytes 1966096 | tf_op jit(solution)/shard_map/all_gather | solution.py:68
  83.3 5.7 %fusion.6 = f32[320,1024]{1,0:T(8,128)S(1)} fusion(bf16[320,3072]{1,0:T(8,128)(2,1)} %all-gather.3.cloned.1.call-done, bf16[1,3072,1024]{2,1,0:T(8,128)(2,1)} %param.14), kind=kOutput, calls=%fused_computation.10 | convolution fusion | flops 2013265920 | bytes 9568256 | tf_op jit(solution)/shard_map/dot_general | solution.py:70
  89.1 5.7 %multiply_convert_fusion.1 = (bf16[320,1024]{1,0:T(8,128)(2,1)S(1)}, bf16[320,1024]{1,0:T(8,128)(2,1)S(1)}, bf16[320,1024]{1,0:T(8,128)(2,1)S(1)}) fusion(f32[320,1024]{1,0:T(8,128)S(1)} %copy-done.6, f32[320,1024]{1,0:T(8,128)S(1)} %fusion.6, bf16[320,3072]{1,0:T(8,128)(2,1)S(1)} %copy-done.4, bf16[1,3072,1024]{2,1,0:T(8,128)(2,1)} %param.13), kind=kOutput, calls=%fused_computation.24 | convolution fusion | flops 2018181120 | bytes 12845056 | tf_op jit(solution)/shard_map/dot_general | solution.py:69
  94.9 2.2 fusion.4
  97.2 2.3 fusion.15
  99.4 2.4 copy.66
  101.9 0.2 reduce-scatter.7.cloned.1.call-start
  102.1 5.0 fusion.18
  107.1 2.4 copy.64
  109.5 34.8 %reduce-scatter.9.cloned.1.call-done = bf16[384,320]{1,0:T(8,128)(2,1)} async-done(((bf16[3072,320]{1,0:T(8,128)(2,1)}), bf16[384,320]{1,0:T(8,128)(2,1)}) %reduce-scatter.9.cloned.1.call-update) | async-done | bytes 245776
  144.4 1.8 copy.67
  146.2 4.6 all-to-all-start.3
  150.8 10.9 %convolution_convert_fusion = bf16[3072,2048]{1,0:T(8,128)(2,1)} fusion(bf16[320,3072]{1,0:T(8,128)(2,1)S(1)} %copy-done.5, bf16[320,1024]{1,0:T(8,128)(2,1)} %copy-done.8, bf16[320,1024]{1,0:T(8,128)(2,1)} %copy-done.7), kind=kOutput, calls=%fused_computation.2 | convolution fusion | flops 4035444736 | bytes 15859712 | tf_op jit(solution)/shard_map/dot_general | solution.py:13
  161.7 28.8 %reduce-scatter.7.cloned.1.call-done = bf16[384,320]{1,0:T(8,128)(2,1)} async-done(((bf16[3072,320]{1,0:T(8,128)(2,1)}), bf16[384,320]{1,0:T(8,128)(2,1)}) %reduce-scatter.7.cloned.1.call-update) | async-done | bytes 245776
  190.5 1.8 copy.65
  192.3 4.6 all-to-all-start.1
  196.9 10.4 %fusion.32 = (bf16[3072,1024]{1,0:T(8,128)(2,1)}, bf16[3072,1024]{1,0:T(8,128)(2,1)}) fusion(bf16[3072,2048]{1,0:T(8,128)(2,1)} %convolution_convert_fusion), kind=kLoop, calls=%fused_computation.55 | loop fusion | bytes 25165824 | tf_op jit(solution)/shard_map/slice | solution.py:119
  207.4 76.9 %all_to_all.70 = bf16[8,384,1024]{2,1,0:T(8,128)(2,1)} all-to-all(bf16[8,384,1024]{2,1,0:T(8,128)(2,1)} %bitcast.69), channel_id=1, replica_groups=mesh['ep'=4,'tp'=8] {'tp'}, dimensions={0} | all-to-all | bytes 12582912 | tf_op jit(solution)/shard_map/all_to_all | solution.py:121
  284.2 4.9 all-to-all-start.5
  289.1 3.7 convolution_convert_fusion.1
  292.8 3.3 copy.72
  296.1 64.6 %all-to-all-done.5 = bf16[8,384,1024]{2,1,0:T(8,128)(2,1)} async-done(((bf16[8,384,1024]{2,1,0:T(8,128)(2,1)}), bf16[8,384,1024]{2,1,0:T(8,128)(2,1)}, u32[]{:S(2)}, u32[]{:S(2)}) %all-to-all-start.5) | async-done | bytes 6291488 | tf_op jit(solution)/shard_map/all_to_all | solution.py:122
  360.7 4.8 all-to-all-start.6
  365.5 1.0 gather_fusion.1
  366.5 1.0 gather_fusion
  367.7 0.2 reshape.111
  367.9 0.2 multiply_reduce_fusion
  368.1 0.1 reduce_sum.61
  368.2 85.9 %psum.7 = f32[96,2]{1,0:T(8,128)S(1)} all-reduce(f32[96,2]{1,0:T(8,128)S(1)} %reduce_sum.61), channel_id=1, replica_groups=mesh['ep'=4,'tp'=8] {'tp'}, use_global_device_ids=true, to_apply=%region_9.11 | all-reduce | flops 192 | bytes 1536 | tf_op jit(solution)/shard_map/psum | solution.py:92
  454.2 0.6 copy.63
  454.8 1.0 reduce_sum.59
  455.8 1.1 multiply_reduce_fusion.1
  456.9 9.0 %copy.60 = bf16[384,8,1024]{2,1,0:T(8,128)(2,1)} copy(bf16[384,8,1024]{2,0,1:T(8,128)(2,1)} %bitcast.66) | data formatting | bytes 12582912 | tf_op jit(solution)/shard_map/all_to_all | solution.py:121
  465.9 10.4 %broadcast_in_dim.15 = bf16[1,384,8192]{2,1,0:T(8,128)(2,1)} reshape(bf16[384,8,1024]{2,1,0:T(8,128)(2,1)} %copy.60) | data formatting | bytes 12582912 | tf_op jit(solution)/shard_map/broadcast_in_dim | solution.py:131
  476.3 9.0 %copy.61 = bf16[384,8,1024]{2,1,0:T(8,128)(2,1)} copy(bf16[384,8,1024]{2,0,1:T(8,128)(2,1)} %bitcast.16) | data formatting | bytes 12582912 | tf_op jit(solution)/shard_map/all_to_all | solution.py:122
  485.3 10.4 %broadcast_in_dim.26 = bf16[1,384,8192]{2,1,0:T(8,128)(2,1)} reshape(bf16[384,8,1024]{2,1,0:T(8,128)(2,1)} %copy.61) | data formatting | bytes 12582912 | tf_op jit(solution)/shard_map/broadcast_in_dim | solution.py:132
  495.7 6.1 %copy.75 = bf16[1,8192,384]{2,1,0:T(8,128)(2,1)} copy(bf16[1,8192,384]{2,1,0:T(8,128)(2,1)} %bitcast.18) | data formatting | bytes 12582912
  (60 shorter events, 1.5 us)
Async XLA Ops:
  7.2 20.3 %copy-start = (bf16[96,384]{1,0:T(8,128)(2,1)S(1)}, bf16[96,384]{1,0:T(8,128)(2,1)}, u32[]{:S(2)}) copy-start(bf16[96,384]{1,0:T(8,128)(2,1)} %param.9) | copy-start | bytes 221188
  7.2 20.2 %copy-start.2 = (s32[96,2]{0,1:T(2,128)S(1)}, s32[96,2]{0,1:T(2,128)}, u32[]{:S(2)}) copy-start(s32[96,2]{0,1:T(2,128)} %param.11) | copy-start | bytes 2308
  7.2 46.7 %all-gather.5.cloned.1.call-start = ((), (), s32[]{:S(2)}) async-start(), calls=%async_computation.10 | async-start | bytes 2211840 | tf_op jit(solution)/shard_map/all_gather | solution.py:93
  27.1 56.2 %all-gather.3.cloned.1.call-start = ((), (), s32[]{:S(2)}) async-start(), calls=%async_computation.9 | async-start | bytes 2211840 | tf_op jit(solution)/shard_map/all_gather | solution.py:68
  38.6 105.8 %reduce-scatter.9.cloned.1.call-start = ((), (), s32[]{:S(2)}) async-start(), calls=%async_computation.12 | async-start | bytes 2654208
  83.3 5.7 %copy-start.4 = (bf16[320,3072]{1,0:T(8,128)(2,1)S(1)}, bf16[320,3072]{1,0:T(8,128)(2,1)}, u32[]{:S(2)}) copy-start(bf16[320,3072]{1,0:T(8,128)(2,1)} %all-gather.3.cloned.1.call-done) | copy-start | bytes 5898244
  83.3 5.7 %copy-start.6 = (f32[320,1024]{1,0:T(8,128)S(1)}, f32[320,1024]{1,0:T(8,128)}, u32[]{:S(2)}) copy-start(f32[320,1024]{1,0:T(8,128)} %fusion) | copy-start | bytes 3932164
  83.3 11.5 %slice-start = ((s8[6291456]{0:T(1024)(128)(4,1)}), s8[4194304]{0:T(1024)(128)(4,1)S(1)}, s32[]{:S(2)}) async-start(s8[6291456]{0:T(1024)(128)(4,1)} %bitcast.83), calls=%async_computation.13 | async-start | bytes 8388608
  83.3 13.8 %slice-start.2 = ((s8[6291456]{0:T(1024)(128)(4,1)}), s8[4194304]{0:T(1024)(128)(4,1)S(1)}, s32[]{:S(2)}) async-start(s8[6291456]{0:T(1024)(128)(4,1)} %bitcast.85), calls=%async_computation.15 | async-start | bytes 8388608
  89.1 5.8 %slice-start.1 = ((s8[6291456]{0:T(1024)(128)(4,1)}), s8[2097152]{0:T(1024)(128)(4,1)S(1)}, s32[]{:S(2)}) async-start(s8[6291456]{0:T(1024)(128)(4,1)} %bitcast.83), calls=%async_computation.14 | async-start | bytes 4194304
  89.1 8.1 %slice-start.3 = ((s8[6291456]{0:T(1024)(128)(4,1)}), s8[2097152]{0:T(1024)(128)(4,1)S(1)}, s32[]{:S(2)}) async-start(s8[6291456]{0:T(1024)(128)(4,1)} %bitcast.85), calls=%async_computation.16 | async-start | bytes 4194304
  94.8 2.3 copy-start.8
  94.8 2.3 copy-start.7
  101.9 88.6 %reduce-scatter.7.cloned.1.call-start = ((), (), s32[]{:S(2)}) async-start(), calls=%async_computation.11 | async-start | bytes 2654208
  109.5 41.3 %copy-start.5 = (bf16[320,3072]{1,0:T(8,128)(2,1)S(1)}, bf16[320,3072]{1,0:T(8,128)(2,1)}, u32[]{:S(2)}) copy-start(bf16[320,3072]{1,0:T(8,128)(2,1)} %all-gather.3.cloned.1.call-done) | copy-start | bytes 5898244
  146.2 46.2 %all-to-all-start.3 = ((bf16[4,80,384]{2,1,0:T(8,128)(2,1)}), bf16[4,80,384]{2,1,0:T(8,128)(2,1)S(1)}, u32[]{:S(2)}, u32[]{:S(2)}) async-start(bf16[4,80,384]{2,1,0:T(8,128)(2,1)} %bitcast.11), calls=%async_computation.3 | async-start | bytes 491520 | tf_op jit(solution)/shard_map/all_to_all | solution.py:103
  192.3 15.0 %all-to-all-start.1 = ((bf16[4,80,384]{2,1,0:T(8,128)(2,1)}), bf16[4,80,384]{2,1,0:T(8,128)(2,1)S(1)}, u32[]{:S(2)}, u32[]{:S(2)}) async-start(bf16[4,80,384]{2,1,0:T(8,128)(2,1)} %bitcast.7), calls=%async_computation.1 | async-start | bytes 491520 | tf_op jit(solution)/shard_map/all_to_all | solution.py:78
  284.2 4.9 copy-start.3
  284.2 76.5 %all-to-all-start.5 = ((bf16[8,384,1024]{2,1,0:T(8,128)(2,1)}), bf16[8,384,1024]{2,1,0:T(8,128)(2,1)}, u32[]{:S(2)}, u32[]{:S(2)}) async-start(bf16[8,384,1024]{2,1,0:T(8,128)(2,1)} %bitcast.68), calls=%async_computation.5 | async-start | bytes 12582912 | tf_op jit(solution)/shard_map/all_to_all | solution.py:122
  360.7 135.0 %all-to-all-start.6 = ((bf16[1024,8,384]{2,0,1:T(8,128)(2,1)}), bf16[1024,8,384]{2,0,1:T(8,128)(2,1)}, u32[]{:S(2)}, u32[]{:S(2)}) async-start(bf16[1024,8,384]{2,0,1:T(8,128)(2,1)} %bitcast.67), calls=%async_computation.6 | async-start | bytes 12582912 | tf_op jit(solution)/shard_map/all_to_all | solution.py:124
  495.7 6.2 %copy-start.1 = (bf16[96,384]{1,0:T(8,128)(2,1)S(1)}, bf16[96,384]{1,0:T(8,128)(2,1)}, u32[]{:S(2)}) copy-start(bf16[96,384]{1,0:T(8,128)(2,1)} %param.9) | copy-start | bytes 221188
Sparse Core Ops, SparseCore 0:
  27.2 26.6 all-gather.4
  55.8 27.5 all-gather.2
  102.0 42.3 reduce-scatter.8
  148.2 42.3 reduce-scatter.6
where the time goes:
time: 510 us; the launch traced here: 508 us
  blocking collectives  188 us (37%)
  waiting for transfers between devices  166 us (33%)
  local copies, waits for them, and re-layouts  73.7 us (14%)
  matrix products  42.8 us (8%)
  starting transfers between devices  19.2 us (4%)
  between operations  14.1 us (3%)
    psum x1, blocking collectives, body(): grad_combine = lax.psum(local_products, 'tp')  85.9 us
    all_to_all x1, blocking collectives, body(): lax.all_to_all(gate_grad, 'tp', split_axis=0, concat_axis=1, tiled=True)  76.9 us
    all_to_all x1, waiting for transfers between devices, body(): lax.all_to_all(up_grad, 'tp', split_axis=0, concat_axis=1, tiled=True)  64.6 us
    unnamed x6, waiting for transfers between devices  63.7 us
    all_gather x1, waiting for transfers between devices, body(): piece = lax.all_gather(recv_rows, 'tp', axis=1, tiled=True)  22.8 us
    unnamed x35, local copies, waits for them, and re-layouts  16.9 us
    all_gather x1, waiting for transfers between devices, body(): lax.all_gather(recv_grad, 'tp', axis=1, tiled=True)  15.3 us
    all_to_all x1, blocking collectives, body(): lax.all_to_all(send_grad.reshape(groups, capacity, piece_width), 'ep', sp...  14.8 us
  transfers between devices with their start and end apart: 8, of which 5 were waited for; matrix products, arithmetic and copies ran while one was open for 18% of the time, Pallas kernels for 0%

commit v1 on v0

--- a/solution.py
+++ b/solution.py
@@ -89,7 +89,7 @@
     )
     mixed = jnp.sum(combine_weights[:, :, None] * out_tokens, axis=1).astype(jnp.bfloat16)
     local_products = jnp.sum(cotangent.astype(jnp.float32)[:, None, :] * out_tokens, axis=2)
-    grad_combine = lax.psum(local_products, "tp")
+    grad_combine = jnp.sum(lax.all_gather(local_products, "tp"), axis=0)
     grad_hidden = contract_cols(lax.all_gather(recv_grad, "tp", axis=1, tiled=True), down_weight)
     down_grad = contract_rows(hidden, lax.all_gather(recv_grad, "tp", axis=1, tiled=True))
     grad_gate_pre = (grad_hidden * up_pre * slope).astype(jnp.bfloat16)

time: 510 us -> 495 us (0.971)
  blocking collectives: 188 us -> 173 us
    psum x1 -> x0, blocking collectives: 85.9 us -> none  [body(): grad_combine = lax.psum(local_products, 'tp')]
    all_gather x0 -> x1, blocking collectives: none -> 70.7 us  [body(): grad_combine = jnp.sum(lax.all_gather(local_products, 'tp'), axis=0)]
    unnamed x35 -> x34, local copies, waits for them, and re-layouts: 16.9 us -> 16.2 us
where the time goes in v1:
time: 495 us; the launch traced here: 493 us
  blocking collectives  173 us (35%)
  waiting for transfers between devices  166 us (34%)
  local copies, waits for them, and re-layouts  73.1 us (15%)
  matrix products  42.8 us (9%)
  starting transfers between devices  19.2 us (4%)
  between operations  14.1 us (3%)
    all_to_all x1, blocking collectives, body(): lax.all_to_all(gate_grad, 'tp', split_axis=0, concat_axis=1, tiled=True)  76.9 us
    all_gather x1, blocking collectives, body(): grad_combine = jnp.sum(lax.all_gather(local_products, 'tp'), axis=0)  70.7 us
    all_to_all x1, waiting for transfers between devices, body(): lax.all_to_all(up_grad, 'tp', split_axis=0, concat_axis=1, tiled=True)  64.6 us
    unnamed x6, waiting for transfers between devices  63.7 us
    all_gather x1, waiting for transfers between devices, body(): piece = lax.all_gather(recv_rows, 'tp', axis=1, tiled=True)  22.8 us
    unnamed x34, local copies, waits for them, and re-layouts  16.2 us
    all_gather x1, waiting for transfers between devices, body(): lax.all_gather(recv_grad, 'tp', axis=1, tiled=True)  15.3 us
    all_to_all x1, blocking collectives, body(): lax.all_to_all(send_grad.reshape(groups, capacity, piece_width), 'ep', sp...  14.8 us
  transfers between devices with their start and end apart: 8, of which 5 were waited for; matrix products, arithmetic and copies ran while one was open for 18% of the time, Pallas kernels for 0%

profile of v1, /device:TPU:0, one launch (start us, length us, event | category | flops | bytes accessed | tf_op | source)
XLA Modules:
  0.0 493.1 jit_solution(14174219294558121443)
XLA Ops:
  7.2 0.8 copy.58
  8.2 1.2 reduce-window.6
  9.9 1.0 mul.83
  10.8 0.2 mul.84
  11.1 0.8 copy.57
  12.0 0.3 convolution_convert_fusion.2
  12.3 14.8 %all_to_all.68 = bf16[4,80,384]{2,1,0:T(8,128)(2,1)} all-to-all(bf16[4,80,384]{2,1,0:T(8,128)(2,1)S(1)} %bitcast.77), channel_id=1, replica_groups=mesh['ep'=4,'tp'=8] {'ep'}, dimensions={0} | all-to-all | bytes 491520 | tf_op jit(solution)/shard_map/all_to_all | solution.py:59
  27.5 0.3 convolution_convert_fusion.3
  27.8 10.8 %all_to_all.69 = bf16[4,80,384]{2,1,0:T(8,128)(2,1)} all-to-all(bf16[4,80,384]{2,1,0:T(8,128)(2,1)S(1)} %bitcast.78), channel_id=1, replica_groups=mesh['ep'=4,'tp'=8] {'ep'}, dimensions={0} | all-to-all | bytes 491520 | tf_op jit(solution)/shard_map/all_to_all | solution.py:52
  38.6 15.3 %all-gather.5.cloned.1.call-done = bf16[320,3072]{1,0:T(8,128)(2,1)} async-done(((bf16[320,384]{1,0:T(8,128)(2,1)}), bf16[320,3072]{1,0:T(8,128)(2,1)}) %all-gather.5.cloned.1.call-update) | async-done | bytes 1966096 | tf_op jit(solution)/shard_map/all_gather | solution.py:93
  53.9 6.7 %fusion = f32[320,1024]{1,0:T(8,128)} fusion(bf16[320,3072]{1,0:T(8,128)(2,1)} %all-gather.5.cloned.1.call-done, bf16[1,1024,3072]{2,1,0:T(8,128)(2,1)} %param.15), kind=kOutput, calls=%fused_computation.4 | convolution fusion | flops 2013265920 | bytes 9568256 | tf_op jit(solution)/shard_map/dot_general | solution.py:19
  60.6 22.8 %all-gather.3.cloned.1.call-done = bf16[320,3072]{1,0:T(8,128)(2,1)} async-done(((bf16[320,384]{1,0:T(8,128)(2,1)}), bf16[320,3072]{1,0:T(8,128)(2,1)}) %all-gather.3.cloned.1.call-update) | async-done | bytes 1966096 | tf_op jit(solution)/shard_map/all_gather | solution.py:68
  83.3 5.7 %fusion.6 = f32[320,1024]{1,0:T(8,128)S(1)} fusion(bf16[320,3072]{1,0:T(8,128)(2,1)} %all-gather.3.cloned.1.call-done, bf16[1,3072,1024]{2,1,0:T(8,128)(2,1)} %param.14), kind=kOutput, calls=%fused_computation.10 | convolution fusion | flops 2013265920 | bytes 9568256 | tf_op jit(solution)/shard_map/dot_general | solution.py:70
  89.1 5.7 %multiply_convert_fusion.1 = (bf16[320,1024]{1,0:T(8,128)(2,1)S(1)}, bf16[320,1024]{1,0:T(8,128)(2,1)S(1)}, bf16[320,1024]{1,0:T(8,128)(2,1)S(1)}) fusion(f32[320,1024]{1,0:T(8,128)S(1)} %copy-done.6, f32[320,1024]{1,0:T(8,128)S(1)} %fusion.6, bf16[320,3072]{1,0:T(8,128)(2,1)S(1)} %copy-done.4, bf16[1,3072,1024]{2,1,0:T(8,128)(2,1)} %param.13), kind=kOutput, calls=%fused_computation.24 | convolution fusion | flops 2018181120 | bytes 12845056 | tf_op jit(solution)/shard_map/dot_general | solution.py:69
  94.9 2.2 fusion.4
  97.2 2.3 fusion.15
  99.4 2.4 copy.71
  101.9 0.2 reduce-scatter.7.cloned.1.call-start
  102.1 5.0 %fusion.18 = bf16[320,3072]{1,0:T(8,128)(2,1)S(1)} fusion(bf16[320,1024]{1,0:T(8,128)(2,1)S(1)} %get-tuple-element.31, bf16[1,1024,3072]{2,1,0:T(8,128)(2,1)} %param.15), kind=kOutput, calls=%fused_computation.19 | convolution fusion | flops 2014248960 | bytes 8912896 | tf_op jit(solution)/shard_map/dot_general | solution.py:74
  107.1 2.4 copy.69
  109.5 34.8 %reduce-scatter.9.cloned.1.call-done = bf16[384,320]{1,0:T(8,128)(2,1)} async-done(((bf16[3072,320]{1,0:T(8,128)(2,1)}), bf16[384,320]{1,0:T(8,128)(2,1)}) %reduce-scatter.9.cloned.1.call-update) | async-done | bytes 245776
  144.4 1.8 copy.72
  146.2 4.6 all-to-all-start.3
  150.8 10.9 %convolution_convert_fusion = bf16[3072,2048]{1,0:T(8,128)(2,1)} fusion(bf16[320,3072]{1,0:T(8,128)(2,1)S(1)} %copy-done.5, bf16[320,1024]{1,0:T(8,128)(2,1)} %copy-done.8, bf16[320,1024]{1,0:T(8,128)(2,1)} %copy-done.7), kind=kOutput, calls=%fused_computation.2 | convolution fusion | flops 4035444736 | bytes 15859712 | tf_op jit(solution)/shard_map/dot_general | solution.py:13
  161.7 28.8 %reduce-scatter.7.cloned.1.call-done = bf16[384,320]{1,0:T(8,128)(2,1)} async-done(((bf16[3072,320]{1,0:T(8,128)(2,1)}), bf16[384,320]{1,0:T(8,128)(2,1)}) %reduce-scatter.7.cloned.1.call-update) | async-done | bytes 245776
  190.5 1.8 copy.70
  192.3 4.6 all-to-all-start.1
  196.9 10.4 %fusion.32 = (bf16[3072,1024]{1,0:T(8,128)(2,1)}, bf16[3072,1024]{1,0:T(8,128)(2,1)}) fusion(bf16[3072,2048]{1,0:T(8,128)(2,1)} %convolution_convert_fusion), kind=kLoop, calls=%fused_computation.55 | loop fusion | bytes 25165824 | tf_op jit(solution)/shard_map/slice | solution.py:119
  207.4 76.9 %all_to_all.70 = bf16[8,384,1024]{2,1,0:T(8,128)(2,1)} all-to-all(bf16[8,384,1024]{2,1,0:T(8,128)(2,1)} %bitcast.69), channel_id=1, replica_groups=mesh['ep'=4,'tp'=8] {'tp'}, dimensions={0} | all-to-all | bytes 12582912 | tf_op jit(solution)/shard_map/all_to_all | solution.py:121
  284.2 4.9 all-to-all-start.5
  289.1 3.7 convolution_convert_fusion.1
  292.8 3.3 copy.78
  296.1 64.6 %all-to-all-done.5 = bf16[8,384,1024]{2,1,0:T(8,128)(2,1)} async-done(((bf16[8,384,1024]{2,1,0:T(8,128)(2,1)}), bf16[8,384,1024]{2,1,0:T(8,128)(2,1)}, u32[]{:S(2)}, u32[]{:S(2)}) %all-to-all-start.5) | async-done | bytes 6291488 | tf_op jit(solution)/shard_map/all_to_all | solution.py:122
  360.7 4.8 all-to-all-start.6
  365.5 1.0 gather_fusion.1
  366.5 1.0 gather_fusion
  367.7 0.2 reshape.112
  367.9 0.2 multiply_reduce_fusion
  368.1 0.1 all_gather.16
  368.3 1.0 reduce_sum.66
  369.3 70.7 %all_gather.17 = f32[8,96,2]{1,2,0:T(2,128)S(1)} all-gather(f32[1,96,2]{1,2,0:T(2,128)S(1)} %copy.63), channel_id=1, replica_groups=mesh['ep'=4,'tp'=8] {'tp'}, dimensions={0}, use_global_device_ids=true | all-gather | bytes 6912 | tf_op jit(solution)/shard_map/all_gather | solution.py:92
  440.0 0.6 reduce_sum.68
  440.6 1.1 multiply_reduce_fusion.1
  441.7 9.0 %copy.65 = bf16[384,8,1024]{2,1,0:T(8,128)(2,1)} copy(bf16[384,8,1024]{2,0,1:T(8,128)(2,1)} %bitcast.66) | data formatting | bytes 12582912 | tf_op jit(solution)/shard_map/all_to_all | solution.py:121
  450.7 10.4 %broadcast_in_dim.15 = bf16[1,384,8192]{2,1,0:T(8,128)(2,1)} reshape(bf16[384,8,1024]{2,1,0:T(8,128)(2,1)} %copy.65) | data formatting | bytes 12582912 | tf_op jit(solution)/shard_map/broadcast_in_dim | solution.py:131
  461.1 9.0 %copy.66 = bf16[384,8,1024]{2,1,0:T(8,128)(2,1)} copy(bf16[384,8,1024]{2,0,1:T(8,128)(2,1)} %bitcast.16) | data formatting | bytes 12582912 | tf_op jit(solution)/shard_map/all_to_all | solution.py:122
  470.0 10.4 %broadcast_in_dim.26 = bf16[1,384,8192]{2,1,0:T(8,128)(2,1)} reshape(bf16[384,8,1024]{2,1,0:T(8,128)(2,1)} %copy.66) | data formatting | bytes 12582912 | tf_op jit(solution)/shard_map/broadcast_in_dim | solution.py:132
  480.4 6.1 %copy.81 = bf16[1,8192,384]{2,1,0:T(8,128)(2,1)} copy(bf16[1,8192,384]{2,1,0:T(8,128)(2,1)} %bitcast.18) | data formatting | bytes 12582912
  (61 shorter events, 1.6 us)
Async XLA Ops:
  7.2 20.3 %copy-start = (bf16[96,384]{1,0:T(8,128)(2,1)S(1)}, bf16[96,384]{1,0:T(8,128)(2,1)}, u32[]{:S(2)}) copy-start(bf16[96,384]{1,0:T(8,128)(2,1)} %param.9) | copy-start | bytes 221188
  7.2 20.2 %copy-start.2 = (s32[96,2]{0,1:T(2,128)S(1)}, s32[96,2]{0,1:T(2,128)}, u32[]{:S(2)}) copy-start(s32[96,2]{0,1:T(2,128)} %param.11) | copy-start | bytes 2308
  7.2 46.7 %all-gather.5.cloned.1.call-start = ((), (), s32[]{:S(2)}) async-start(), calls=%async_computation.10 | async-start | bytes 2211840 | tf_op jit(solution)/shard_map/all_gather | solution.py:93
  27.1 56.2 %all-gather.3.cloned.1.call-start = ((), (), s32[]{:S(2)}) async-start(), calls=%async_computation.9 | async-start | bytes 2211840 | tf_op jit(solution)/shard_map/all_gather | solution.py:68
  38.6 105.8 %reduce-scatter.9.cloned.1.call-start = ((), (), s32[]{:S(2)}) async-start(), calls=%async_computation.12 | async-start | bytes 2654208
  83.3 5.7 %copy-start.4 = (bf16[320,3072]{1,0:T(8,128)(2,1)S(1)}, bf16[320,3072]{1,0:T(8,128)(2,1)}, u32[]{:S(2)}) copy-start(bf16[320,3072]{1,0:T(8,128)(2,1)} %all-gather.3.cloned.1.call-done) | copy-start | bytes 5898244
  83.3 5.7 %copy-start.6 = (f32[320,1024]{1,0:T(8,128)S(1)}, f32[320,1024]{1,0:T(8,128)}, u32[]{:S(2)}) copy-start(f32[320,1024]{1,0:T(8,128)} %fusion) | copy-start | bytes 3932164
  83.3 11.5 %slice-start = ((s8[6291456]{0:T(1024)(128)(4,1)}), s8[4194304]{0:T(1024)(128)(4,1)S(1)}, s32[]{:S(2)}) async-start(s8[6291456]{0:T(1024)(128)(4,1)} %bitcast.83), calls=%async_computation.13 | async-start | bytes 8388608
  83.3 13.8 %slice-start.2 = ((s8[6291456]{0:T(1024)(128)(4,1)}), s8[4194304]{0:T(1024)(128)(4,1)S(1)}, s32[]{:S(2)}) async-start(s8[6291456]{0:T(1024)(128)(4,1)} %bitcast.85), calls=%async_computation.15 | async-start | bytes 8388608
  89.1 5.8 %slice-start.1 = ((s8[6291456]{0:T(1024)(128)(4,1)}), s8[2097152]{0:T(1024)(128)(4,1)S(1)}, s32[]{:S(2)}) async-start(s8[6291456]{0:T(1024)(128)(4,1)} %bitcast.83), calls=%async_computation.14 | async-start | bytes 4194304
  89.1 8.1 %slice-start.3 = ((s8[6291456]{0:T(1024)(128)(4,1)}), s8[2097152]{0:T(1024)(128)(4,1)S(1)}, s32[]{:S(2)}) async-start(s8[6291456]{0:T(1024)(128)(4,1)} %bitcast.85), calls=%async_computation.16 | async-start | bytes 4194304
  94.8 2.3 copy-start.8
  94.8 2.3 copy-start.7
  101.9 88.6 %reduce-scatter.7.cloned.1.call-start = ((), (), s32[]{:S(2)}) async-start(), calls=%async_computation.11 | async-start | bytes 2654208
  109.5 41.3 %copy-start.5 = (bf16[320,3072]{1,0:T(8,128)(2,1)S(1)}, bf16[320,3072]{1,0:T(8,128)(2,1)}, u32[]{:S(2)}) copy-start(bf16[320,3072]{1,0:T(8,128)(2,1)} %all-gather.3.cloned.1.call-done) | copy-start | bytes 5898244
  146.2 46.2 %all-to-all-start.3 = ((bf16[4,80,384]{2,1,0:T(8,128)(2,1)}), bf16[4,80,384]{2,1,0:T(8,128)(2,1)S(1)}, u32[]{:S(2)}, u32[]{:S(2)}) async-start(bf16[4,80,384]{2,1,0:T(8,128)(2,1)} %bitcast.11), calls=%async_computation.3 | async-start | bytes 491520 | tf_op jit(solution)/shard_map/all_to_all | solution.py:103
  192.3 15.0 %all-to-all-start.1 = ((bf16[4,80,384]{2,1,0:T(8,128)(2,1)}), bf16[4,80,384]{2,1,0:T(8,128)(2,1)S(1)}, u32[]{:S(2)}, u32[]{:S(2)}) async-start(bf16[4,80,384]{2,1,0:T(8,128)(2,1)} %bitcast.7), calls=%async_computation.1 | async-start | bytes 491520 | tf_op jit(solution)/shard_map/all_to_all | solution.py:78
  284.2 4.9 copy-start.3
  284.2 76.5 %all-to-all-start.5 = ((bf16[8,384,1024]{2,1,0:T(8,128)(2,1)}), bf16[8,384,1024]{2,1,0:T(8,128)(2,1)}, u32[]{:S(2)}, u32[]{:S(2)}) async-start(bf16[8,384,1024]{2,1,0:T(8,128)(2,1)} %bitcast.68), calls=%async_computation.5 | async-start | bytes 12582912 | tf_op jit(solution)/shard_map/all_to_all | solution.py:122
  360.7 119.8 %all-to-all-start.6 = ((bf16[1024,8,384]{2,0,1:T(8,128)(2,1)}), bf16[1024,8,384]{2,0,1:T(8,128)(2,1)}, u32[]{:S(2)}, u32[]{:S(2)}) async-start(bf16[1024,8,384]{2,0,1:T(8,128)(2,1)} %bitcast.67), calls=%async_computation.6 | async-start | bytes 12582912 | tf_op jit(solution)/shard_map/all_to_all | solution.py:124
  480.4 6.2 %copy-start.1 = (bf16[96,384]{1,0:T(8,128)(2,1)S(1)}, bf16[96,384]{1,0:T(8,128)(2,1)}, u32[]{:S(2)}) copy-start(bf16[96,384]{1,0:T(8,128)(2,1)} %param.9) | copy-start | bytes 221188
Sparse Core Ops, SparseCore 0:
  27.2 26.6 all-gather.4
  55.8 27.5 all-gather.2
  102.0 42.3 reduce-scatter.8
  148.2 42.3 reduce-scatter.6
